TPU v7x, 32 devices: a whole 2x2x4 slice. The times are simulated.
32 devices in a mesh: seq: 16 (over z, y, core), tp: 2 (over x).
Axes of the slice: x: 2, y: 2, z: 4, core: 2. Of those that a mesh axis runs over, the one named last changes fastest.
Arguments:
- video_query: bfloat16 [2, 8192, 3072], P(None, 'seq', 'tp'), may hold values from -2048 to 2048
- text_states: bfloat16 [2, 256, 4096], P(None, 'seq'), may hold values from -24 to 24
- key_weight: bfloat16 [4096, 3072], P(None, 'tp'), may hold values from -1 to 1
- value_weight: bfloat16 [4096, 3072], P(None, 'tp'), may hold values from -0.09375 to 0.09375
- text_lengths: int32 [2], replicated, may hold values from 64 to 256, as said below
- output_grad: bfloat16 [2, 8192, 3072], P(None, 'seq', 'tp'), may hold values from -6 to 6
Outputs:
- attended: bfloat16 [2, 8192, 3072], P(None, 'seq', 'tp')
- query_grad: bfloat16 [2, 8192, 3072], P(None, 'seq', 'tp')
- key_weight_grad: float32 [4096, 3072], P('seq', 'tp')
- value_weight_grad: float32 [4096, 3072], P('seq', 'tp')
Inputs may be any that keep to these rules, and one draw needn't show every extreme that they name: Keys of sample b at text positions from text_lengths[b] on are masked; one sample has all 256 text tokens.
All inputs are finite; a program needn't handle non-finite values.
Results may differ from a plain program's by a relative error of at most 0.012.
The roundings to bfloat16 on the way count: a program that leaves them out, or rounds other values in their place, can miss the bound.
Values may be sent and summed in bfloat16 or wider, within the bound.
A program may use at most 128 MiB of HBM per device.

v0:
```python
import math

import jax
import jax.numpy as jnp
from jax import lax
from jax.sharding import PartitionSpec as P

DT = 4096
HEADS = 24
HEAD = 128


def split_product(text_low, gradients):
    leading = lax.optimization_barrier(gradients.astype(jnp.bfloat16))
    remainder = (gradients - leading.astype(jnp.float32)).astype(jnp.bfloat16)
    dimensions = (((0,), (0,)), ((), ()))
    first = lax.dot_general(text_low, leading, dimensions, preferred_element_type=jnp.float32)
    second = lax.dot_general(text_low, remainder, dimensions, preferred_element_type=jnp.float32)
    return first + second


def per_device(video_query, text_states, key_weight, value_weight, text_lengths, output_grad):
    samples, video_rows, feature_count = video_query.shape
    head_count = feature_count // HEAD
    scaling = 1.0 / math.sqrt(HEAD)
    text_full = lax.all_gather(text_states, "seq", axis=1, tiled=True)
    key_states = jnp.dot(text_full, key_weight, preferred_element_type=jnp.float32).astype(
        jnp.bfloat16
    )
    value_states = jnp.dot(text_full, value_weight, preferred_element_type=jnp.float32).astype(
        jnp.bfloat16
    )
    text_count = key_states.shape[1]
    query_heads = video_query.reshape(samples, video_rows, head_count, HEAD)
    key_heads = key_states.reshape(samples, text_count, head_count, HEAD)
    value_heads = value_states.reshape(samples, text_count, head_count, HEAD)
    grad_heads = output_grad.reshape(samples, video_rows, head_count, HEAD)
    scores = (
        jnp.einsum("bthe,blhe->bhtl", query_heads, key_heads, preferred_element_type=jnp.float32)
        * scaling
    )
    allowed = jnp.arange(text_count)[None, None, None, :] < text_lengths[:, None, None, None]
    scores = jnp.where(allowed, scores, -1e30)
    highest = jnp.max(scores, axis=-1, keepdims=True)
    weights = jnp.exp(scores - highest)
    probs = weights / jnp.sum(weights, axis=-1, keepdims=True)
    probs_low = probs.astype(jnp.bfloat16)
    attended = jnp.einsum(
        "bhtl,blhe->bthe", probs_low, value_heads, preferred_element_type=jnp.float32
    )
    attended = attended.astype(jnp.bfloat16).reshape(samples, video_rows, feature_count)
    dprob = jnp.einsum(
        "bthe,blhe->bhtl", grad_heads, value_heads, preferred_element_type=jnp.float32
    )
    delta = jnp.sum(probs * dprob, axis=-1, keepdims=True)
    dscore = (probs * (dprob - delta) * scaling).astype(jnp.bfloat16)
    query_grad = jnp.einsum(
        "bhtl,blhe->bthe", dscore, key_heads, preferred_element_type=jnp.float32
    )
    query_grad = query_grad.astype(jnp.bfloat16).reshape(samples, video_rows, feature_count)
    key_grad = jnp.einsum(
        "bhtl,bthe->blhe", dscore, query_heads, preferred_element_type=jnp.float32
    )
    key_grad = key_grad.reshape(samples, text_count, feature_count)
    value_grad = jnp.einsum(
        "bhtl,bthe->blhe", probs_low, grad_heads, preferred_element_type=jnp.float32
    )
    value_grad = value_grad.reshape(samples, text_count, feature_count)
    key_total, value_total = lax.psum((key_grad, value_grad), "seq")
    columns = lax.all_to_all(text_states, "seq", split_axis=2, concat_axis=1, tiled=True)
    stacked = jnp.concatenate([key_total, value_total], axis=-1).reshape(
        samples * text_count, 2 * feature_count
    )
    columns_flat = columns.reshape(samples * text_count, -1)
    summed = split_product(columns_flat, stacked)
    squares = jnp.sum(summed * summed)
    overall = lax.psum(squares, ("seq", "tp"))
    spread = jnp.sqrt(overall / (2.0 * DT * HEADS * HEAD) + 1e-06)
    factor = 1.0 / jnp.maximum(spread, 1.0)
    return (
        attended,
        query_grad,
        summed[:, :feature_count] * factor,
        summed[:, feature_count:] * factor,
    )


def solution(mesh):
    in_specs = (
        P(None, "seq", "tp"),
        P(None, "seq", None),
        P(None, "tp"),
        P(None, "tp"),
        P(),
        P(None, "seq", "tp"),
    )
    out_specs = (P(None, "seq", "tp"), P(None, "seq", "tp"), P("seq", "tp"), P("seq", "tp"))
    return jax.shard_map(
        per_device, mesh=mesh, in_specs=in_specs, out_specs=out_specs, check_vma=False
    )
```

profile of v0, /device:TPU:0, one launch (start us, length us, event | category | flops | bytes accessed | tf_op | source)
XLA Modules:
  0.0 351.1 jit_solution(5138587056094816315)
XLA Ops:
  7.2 0.0 all-gather.2.cloned.1.call-start
  7.2 0.7 all-gather.2.cloned.1.call-update
  7.9 0.0 all-reduce.3.cloned.1.call-start
  7.9 4.6 %copy.65 = bf16[2,512,1536]{1,2,0:T(8,128)(2,1)} copy(bf16[2,512,1536]{2,1,0:T(8,128)(2,1)} %param.6) | data formatting | bytes 6291456 | tf_op args[0]
  12.6 0.0 copy-start.4
  12.6 3.2 copy.69
  15.8 0.0 copy-done.4
  15.8 0.1 iota_compare_fusion
  15.9 47.5 %all-gather.2.cloned.1.call-done = bf16[2,256,4096]{2,1,0:T(8,128)(2,1)} async-done(((bf16[2,16,4096]{2,1,0:T(8,128)(2,1)}), bf16[2,256,4096]{2,1,0:T(8,128)(2,1)}) %all-gather.2.cloned.1.call-update) | async-done | bytes 4194320 | tf_op jit(solution)/shard_map/all_gather | solution.py:26
  63.3 11.7 %fusion.25 = bf16[2,256,1536]{2,1,0:T(8,128)(2,1)} fusion(bf16[2,256,4096]{2,1,0:T(8,128)(2,1)} %all-gather.2.cloned.1.call-done, bf16[4096,1536]{1,0:T(8,128)(2,1)} %param.9), kind=kOutput, calls=%fused_computation.34 | convolution fusion | flops 6443237376 | bytes 18350080 | tf_op jit(solution)/shard_map/dot_general | solution.py:30
  75.1 2.6 copy.63
  77.6 11.8 %fusion.28 = bf16[2,256,1536]{2,1,0:T(8,128)(2,1)} fusion(bf16[2,256,4096]{2,1,0:T(8,128)(2,1)} %all-gather.2.cloned.1.call-done, bf16[4096,1536]{1,0:T(8,128)(2,1)} %param.8), kind=kOutput, calls=%fused_computation.35 | convolution fusion | flops 6443237376 | bytes 18350080 | tf_op jit(solution)/shard_map/dot_general | solution.py:27
  89.5 2.6 copy.64
  92.1 7.7 %fusion.44 = f32[2,12,256,512]{3,2,1,0:T(8,128)} fusion(bf16[2,256,12,128]{1,3,2,0:T(8,128)(2,1)} %bitcast.97, bf16[2,512,12,128]{1,3,2,0:T(8,128)(2,1)S(1)} %bitcast.93), kind=kOutput, calls=%fused_computation.49 | convolution fusion | flops 805306368 | bytes 17301504 | tf_op jit(solution)/shard_map/bthe,blhe->bhtl/dot_general | solution.py:52
  99.8 12.2 %fusion.43 = (f32[2,12,512]{2,1,0:T(8,128)S(1)}, f32[2,12,512,256]{2,3,1,0:T(8,128)}) fusion(pred[2,256]{1,0:T(4,128)(4,1)S(1)} %iota_compare_fusion, bf16[2,256,12,128]{1,3,2,0:T(8,128)(2,1)} %bitcast.107, bf16[2,512,12,128]{1,3,2,0:T(8,128)(2,1)} %bitcast.99), kind=kOutput, calls=%fused_computation.48 | convolution fusion | flops 817889536 | bytes 17351168 | tf_op jit(solution)/shard_map/sub | solution.py:45
  111.9 8.5 %fusion.21 = f32[2,12,256,128]{2,3,1,0:T(8,128)} fusion(bf16[2,512,12,128]{1,3,2,0:T(8,128)(2,1)S(1)} %bitcast.94, f32[2,12,512,256]{2,3,1,0:T(8,128)} %get-tuple-element.25, f32[2,12,512]{2,1,0:T(8,128)S(1)} %get-tuple-element.24), kind=kOutput, calls=%fused_computation.30 | convolution fusion | flops 811597824 | bytes 18923520 | tf_op jit(solution)/shard_map/bhtl,bthe->blhe/dot_general | solution.py:65
  120.4 19.8 %fusion.18 = f32[2,12,256,128]{2,3,1,0:T(8,128)} fusion(bf16[2,512,12,128]{1,3,2,0:T(8,128)(2,1)} %bitcast.100, f32[2,12,256,512]{3,2,1,0:T(8,128)} %fusion.44, f32[2,12,512,256]{2,3,1,0:T(8,128)} %get-tuple-element.25, f32[2,12,512]{2,1,0:T(8,128)S(1)} %get-tuple-element.24), kind=kOutput, calls=%fused_computation.25 | convolution fusion | flops 827339008 | bytes 31506432 | tf_op jit(solution)/shard_map/bhtl,bthe->blhe/dot_general | solution.py:61
  140.2 0.0 copy-start.2
  140.2 3.8 %copy.74 = f32[2,256,1536]{2,1,0:T(8,128)} copy(f32[2,256,1536]{1,2,0:T(8,128)} %bitcast.104) | data formatting | bytes 6291456 | tf_op jit(solution)/shard_map/reshape | solution.py:64
  144.0 0.0 copy-done.2
  144.0 2.4 copy.76
  146.4 0.0 copy-start.3
  146.4 0.0 all-reduce.3.cloned.1.call-update
  146.4 0.9 copy-done.3
  147.3 2.7 copy.77
  150.0 2.4 reshape.75
  152.4 17.7 %all_to_all.15 = bf16[16,2,4096]{2,1,0:T(2,128)(2,1)S(1)} all-to-all(bf16[16,2,4096]{2,1,0:T(2,128)(2,1)S(1)} %reshape.75), channel_id=1, replica_groups=mesh['seq'=16,'tp'=2] {'seq'}, dimensions={0} | all-to-all | bytes 524288 | tf_op jit(solution)/shard_map/all_to_all | solution.py:70
  170.1 1.4 reshape.76
  171.5 1.3 copy.93
  172.8 22.3 %fusion.31 = bf16[2,12,128,512]{3,2,1,0:T(8,128)(2,1)} fusion(bf16[2,256,12,128]{1,3,2,0:T(8,128)(2,1)} %bitcast.108, f32[2,12,256,512]{3,2,1,0:T(8,128)} %fusion.44, f32[2,12,512,256]{2,3,1,0:T(8,128)} %get-tuple-element.25, f32[2,12,512]{2,1,0:T(8,128)S(1)} %get-tuple-element.24), kind=kOutput, calls=%fused_computation.36 | convolution fusion | flops 828911872 | bytes 29933568 | tf_op jit(solution)/shard_map/bhtl,blhe->bthe/dot_general | solution.py:57
  195.1 0.0 copy-start
  195.1 4.8 %copy.81 = bf16[2,512,1536]{2,1,0:T(8,128)(2,1)} copy(bf16[2,512,1536]{1,2,0:T(8,128)(2,1)} %bitcast.103) | data formatting | bytes 6291456
  199.9 0.0 copy-done
  199.9 7.6 %fusion.32 = bf16[2,12,128,512]{3,2,1,0:T(8,128)(2,1)} fusion(bf16[2,256,12,128]{1,3,2,0:T(8,128)(2,1)S(1)} %bitcast.98, f32[2,12,512,256]{2,3,1,0:T(8,128)} %get-tuple-element.25, f32[2,12,512]{2,1,0:T(8,128)S(1)} %get-tuple-element.24), kind=kOutput, calls=%fused_computation.37 | convolution fusion | flops 813170688 | bytes 17350656 | tf_op jit(solution)/shard_map/bhtl,blhe->bthe/dot_general | solution.py:48
  207.4 4.6 %copy.80 = bf16[2,512,1536]{2,1,0:T(8,128)(2,1)} copy(bf16[2,512,1536]{1,2,0:T(8,128)(2,1)} %bitcast.102) | data formatting | bytes 6291456
  212.1 77.0 %all-reduce.3.cloned.1.call-done = (f32[2,256,1536]{2,1,0:T(8,128)}, f32[2,256,1536]{2,1,0:T(8,128)}) async-done(((f32[2,256,1536]{2,1,0:T(8,128)}, f32[2,256,1536]{2,1,0:T(8,128)}), (f32[2,256,1536]{2,1,0:T(8,128)}, f32[2,256,1536]{2,1,0:T(8,128)})) %all-reduce.3.cloned.1.call-update) | async-done | bytes 6291472 | tf_op jit(solution)/shard_map/psum | solution.py:69
  289.1 3.3 pad_maximum_fusion
  292.4 0.4 bitcast_convert_fusion
  292.8 1.0 fusion.13
  293.9 1.0 fusion.45
  294.9 1.6 multiply_reduce_fusion
  296.5 40.4 %psum.23 = f32[]{:T(128)} all-reduce(f32[]{:T(128)} %get-tuple-element.26), channel_id=1, replica_groups=mesh['seq'=16,'tp'=2] {'seq','tp'}, use_global_device_ids=true, to_apply=%region_6.7 | all-reduce | flops 1 | bytes 8 | tf_op jit(solution)/shard_map/psum | solution.py:77
  337.7 1.9 slice_multiply_fusion
  339.5 0.0 copy-start.1
  339.5 3.1 copy.83
  342.7 0.0 copy-done.1
  342.7 1.6 copy.82
Async XLA Ops:
  7.2 56.2 %all-gather.2.cloned.1.call-start = ((), (), s32[]{:S(2)}) async-start(), calls=%async_computation.1 | async-start | bytes 4456448 | tf_op jit(solution)/shard_map/all_gather | solution.py:26
  7.9 281.2 %all-reduce.3.cloned.1.call-start = ((), (), s32[]{:S(2)}) async-start(), calls=%async_computation.2 | async-start | bytes 12582912 | tf_op jit(solution)/shard_map/psum | solution.py:69
  12.6 3.2 copy-start.4
  140.2 3.8 %copy-start.2 = (f32[2,12,256,128]{2,3,1,0:T(8,128)S(1)}, f32[2,12,256,128]{2,3,1,0:T(8,128)}, u32[]{:S(2)}) copy-start(f32[2,12,256,128]{2,3,1,0:T(8,128)} %fusion.21) | copy-start | bytes 9437188
  146.4 0.9 copy-start.3
  195.1 4.8 %copy-start = (bf16[2,256,1536]{1,2,0:T(8,128)(2,1)S(1)}, bf16[2,256,1536]{1,2,0:T(8,128)(2,1)}, u32[]{:S(2)}) copy-start(bf16[2,256,1536]{1,2,0:T(8,128)(2,1)} %copy.63) | copy-start | bytes 4718596
  339.5 3.1 copy-start.1
Sparse Core Ops, SparseCore 0:
  10.2 53.1 all-gather.1
  146.5 142.4 all-reduce.2
where the time goes:
time: 352 us; the launch traced here: 351 us
  waiting for transfers between devices  125 us (36%)
  matrix products  104 us (30%)
  blocking collectives  58.1 us (17%)
  local copies, waits for them, and re-layouts  42.1 us (12%)
  between operations  14.9 us (4%)
  other arithmetic  6.73 us (2%)
    psum x1, waiting for transfers between devices, per_device(): key_total, value_total = lax.psum((key_grad, value_grad), 'seq')  77 us
    all_gather x1, waiting for transfers between devices, per_device(): text_full = lax.all_gather(text_states, 'seq', axis=1, tiled=True)  47.5 us
    psum x1, blocking collectives, per_device(): overall = lax.psum(squares, ('seq', 'tp'))  40.4 us
    unnamed x19, local copies, waits for them, and re-layouts  29.5 us
    dot_general x1, matrix products, per_device(): jnp.einsum('bhtl,blhe->bthe', dscore, key_heads, preferred_element_type=j...  22.3 us
    dot_general x1, matrix products, per_device(): jnp.einsum('bhtl,bthe->blhe', dscore, query_heads, preferred_element_type...  19.8 us
    all_to_all x1, blocking collectives, per_device(): lax.all_to_all(text_states, 'seq', split_axis=2, concat_axis=1, tiled=True)  17.7 us
    sub x1, matrix products, per_device(): weights = jnp.exp(scores - highest)  12.2 us
  transfers between devices with their start and end apart: 2, of which 2 were waited for; matrix products, arithmetic and copies ran while one was open for 16% of the time, Pallas kernels for 0%

commit v1 on v0

v1 whole, which is shorter than its diff:
```python
import functools
import math

import jax
import jax.numpy as jnp
from jax import lax
from jax.experimental import pallas as pl
from jax.experimental.pallas import tpu as pltpu
from jax.sharding import PartitionSpec as P

HEAD = 128
MESH = pl.DeviceIdType.MESH
NEG = -1e30


def rem(a, b):
    return lax.rem(a, b)


class Place:
    def __init__(self, n):
        self.C = 2
        self.Y = 2
        self.Z = n // 4
        self.n = n
        me = lax.axis_index("seq")
        self.me = me
        self.tp = lax.axis_index("tp")
        self.c = rem(me, 2)
        self.y = rem(me // 2, 2)
        self.z = me // 4

    def dev(self, z, y, c):
        return ((z * self.Y + y) * self.C + c, self.tp)

    def core_peer(self):
        return self.dev(self.z, self.y, 1 - self.c)

    def y_peer(self):
        return self.dev(self.z, 1 - self.y, self.c)

    def z_ahead(self, d):
        return rem(self.z + d, self.Z)

    def z_behind(self, d):
        return rem(self.z + self.Z - d, self.Z)

    def z_peer(self, d):
        return self.dev(self.z_ahead(d), self.y, self.c)


def rcopy(src, dst, ssem, rsem, dev):
    return pltpu.make_async_remote_copy(
        src_ref=src, dst_ref=dst, send_sem=ssem, recv_sem=rsem, device_id=dev, device_id_type=MESH
    )


def greet(devices):
    barrier = pltpu.get_barrier_semaphore()
    for d in devices:
        pl.semaphore_signal(barrier, inc=1, device_id=d, device_id_type=MESH)
    pl.semaphore_wait(barrier, len(devices))


class Gather:
    def __init__(self, pos, block, own, ss, rs):
        self.pos, self.block, self.own, self.ss, self.rs = pos, block, own, ss, rs
        self.sent = []

    def copy(self, src, z, y, c, k, dev):
        d = rcopy(src, self.block(z, y, c), self.ss(k), self.rs(k), dev)
        return d

    def go(self, src, z, y, c, k, dev):
        d = self.copy(src, z, y, c, k, dev)
        d.start()
        self.sent.append(d)

    def start(self):
        p = self.pos
        for d in range(p.Z - 1, 0, -1):
            self.go(self.own, p.z, p.y, p.c, d - 1, p.z_peer(d))
        self.go(self.own, p.z, p.y, p.c, p.Z - 1, p.y_peer())
        self.go(self.own, p.z, p.y, p.c, 2 * p.Z - 1, p.core_peer())

    def arrive_z(self, d):
        p = self.pos
        self.sent[p.Z - 1 - d].wait_recv()
        zz = p.z_behind(d)
        self.go(self.block(zz, p.y, p.c), zz, p.y, p.c, p.Z - 1 + d, p.y_peer())
        self.go(self.block(zz, p.y, p.c), zz, p.y, p.c, 2 * p.Z - 1 + d, p.core_peer())

    def arrive_y(self, d):
        p = self.pos
        zz = p.z_behind(d)
        src = self.block(zz, 1 - p.y, p.c)
        rcopy(src, src, self.ss(p.Z - 1 + d), self.rs(p.Z - 1 + d), p.y_peer()).wait_recv()
        self.go(src, zz, 1 - p.y, p.c, 3 * p.Z - 1 + d, p.core_peer())

    def finish(self):
        p = self.pos
        for d in range(2 * p.Z):
            k = 2 * p.Z - 1 + d
            src = self.own
            rcopy(src, src, self.ss(k), self.rs(k), p.core_peer()).wait_recv()
        for d in self.sent:
            d.wait_send()


def gather_kernel(n, k_loc, v_loc, text, k_out, v_out, cols, gs, gr, ts, tr):
    p = Place(n)
    width = cols.shape[-1]
    greet([(rem(p.me + d, n), p.tp) for d in range(1, n)])
    flows = []
    for i, (loc, out) in enumerate(((k_loc, k_out), (v_loc, v_out))):
        f = Gather(
            p,
            lambda z, y, c, out=out: out.at[z, y, c],
            loc,
            lambda k, i=i: gs.at[i, k],
            lambda k, i=i: gr.at[i, k],
        )
        f.start()
        flows.append(f)
    direct = []
    for d in range(1, n):
        to = rem(p.me + d, n)
        start = pl.multiple_of(to * width, 128)
        cp = rcopy(
            text.at[:, :, pl.ds(start, width)], cols.at[p.me], ts.at[d - 1], tr.at[d - 1], (to, p.tp)
        )
        cp.start()
        direct.append(cp)
    k_out[p.z, p.y, p.c] = k_loc[...]
    v_out[p.z, p.y, p.c] = v_loc[...]
    cols[p.me] = text[:, :, pl.ds(pl.multiple_of(p.me * width, 128), width)]
    for d in range(1, p.Z):
        for f in flows:
            f.arrive_z(d)
    for d in range(p.Z):
        for f in flows:
            f.arrive_y(d)
    for f in flows:
        f.finish()
    for cp in direct:
        cp.wait()


def reduce_kernel(n, gk, gv, tk, tv, s1k, s1v, r1k, r1v, s2k, s2v, r2k, r2v, r3k, r3v, own_k, own_v,
                  ss, rs, gs, gr):
    p = Place(n)
    Z = p.Z
    width = gk.shape[-1]
    cut = 2 if width % 256 == 0 else 1
    step = width // cut
    chunks = []
    for h in range(cut):
        for refs in ((gk, tk, s1k, r1k, s2k, r2k, r3k, own_k), (gv, tv, s1v, r1v, s2v, r2v, r3v, own_v)):
            chunks.append((refs, pl.ds(h * step, step)))
    greet([p.core_peer(), p.y_peer()] + [p.z_peer(d) for d in range(1, Z)])
    f32, low = jnp.float32, jnp.bfloat16
    first = []
    for i, ((g, t, s1, r1, s2, r2, r3, own), w) in enumerate(chunks):
        cp = rcopy(
            g.at[:, :, 1 - p.c, :, :, w], r1.at[:, :, :, :, w], ss.at[i, 0], rs.at[i, 0], p.core_peer()
        )
        cp.start()
        first.append(cp)
    second = []
    for i, ((g, t, s1, r1, s2, r2, r3, own), w) in enumerate(chunks):
        first[i].wait_recv()
        for yy in (1 - p.y, p.y):
            s1[:, yy, :, :, w] = (
                g[:, yy, p.c, :, :, w].astype(f32) + r1[:, yy, :, :, w].astype(f32)
            ).astype(low)
            if yy is not p.y:
                cp = rcopy(
                    s1.at[:, 1 - p.y, :, :, w], r2.at[:, :, :, w], ss.at[i, 1], rs.at[i, 1], p.y_peer()
                )
                cp.start()
                second.append(cp)
    third = []
    for i, ((g, t, s1, r1, s2, r2, r3, own), w) in enumerate(chunks):
        second[i].wait_recv()
        mine = []
        for d in range(Z - 1, 0, -1):
            zz = p.z_ahead(d)
            s2[zz, :, :, w] = (
                s1[zz, p.y, :, :, w].astype(f32) + r2[zz, :, :, w].astype(f32)
            ).astype(low)
            cp = rcopy(
                s2.at[zz, :, :, w], r3.at[d - 1, :, :, w], ss.at[i, 1 + d], rs.at[i, 1 + d], p.z_peer(d)
            )
            cp.start()
            mine.append(cp)
        third.append(mine)
    flows = []
    for i, ((g, t, s1, r1, s2, r2, r3, own), w) in enumerate(chunks):
        total = s1[p.z, p.y, :, :, w].astype(f32) + r2[p.z, :, :, w].astype(f32)
        for cp in third[i]:
            cp.wait_recv()
        for d in range(1, Z):
            total = total + r3[d - 1, :, :, w].astype(f32)
        own[:, :, w] = total.astype(low)
        f = Gather(
            p,
            lambda z, y, c, t=t, w=w: t.at[z, y, c, :, :, w],
            own.at[:, :, w],
            lambda k, i=i: gs.at[i, k],
            lambda k, i=i: gr.at[i, k],
        )
        f.start()
        t[p.z, p.y, p.c, :, :, w] = total.astype(low)
        flows.append(f)
    for f in flows:
        for d in range(1, Z):
            f.arrive_z(d)
    for f in flows:
        for d in range(Z):
            f.arrive_y(d)
    for f in flows:
        f.finish()
    for cp in first + second + [c for m in third for c in m]:
        cp.wait_send()


def scalar_kernel(n, m, x, out, ss, rs):
    me, tp = lax.axis_index("seq"), lax.axis_index("tp")
    flat = me * m + tp
    peers = []
    for d in range(1, n * m):
        to = rem(flat + d, n * m)
        peers.append((to // m, rem(to, m)))
    greet(peers)
    copies = []
    for d, dev in enumerate(peers):
        cp = rcopy(x, out.at[flat], ss.at[d], rs.at[d], dev)
        cp.start()
        copies.append(cp)
    out[flat] = x[...]
    for cp in copies:
        cp.wait()


def flat_rows(x):
    n, r, e = x.shape
    if r % 16 == 0:
        return x.reshape(n * r, e)
    return x.astype(jnp.float32).reshape(n * r, e).astype(x.dtype)


def attention_kernel(scaling, lengths, q_ref, k_ref, v_ref, g_ref, a_ref, qg_ref, kg_ref, vg_ref):
    f32, low = jnp.float32, jnp.bfloat16
    length = lengths[pl.program_id(0)]
    q, g = q_ref[0], g_ref[0]
    k, v = flat_rows(k_ref[:, 0]), flat_rows(v_ref[:, 0])
    n, _, r, e = k_ref.shape
    last = (((1,), (1,)), ((), ()))
    head = (((0,), (0,)), ((), ()))
    s = lax.dot_general(k, q, last, preferred_element_type=f32)
    dp = lax.dot_general(v, g, last, preferred_element_type=f32)
    row = lax.broadcasted_iota(jnp.int32, s.shape, 0)
    s = jnp.where(row < length, s, NEG)
    top = jnp.max(s, axis=0, keepdims=True)
    w = jnp.exp2((s - top) * (scaling * math.log2(math.e)))
    inv = 1.0 / jnp.sum(w, axis=0, keepdims=True)
    probs = w * inv
    probs_low = probs.astype(low)
    delta = jnp.sum(probs * dp, axis=0, keepdims=True)
    ds = (probs * (dp - delta) * scaling).astype(low)
    a_ref[0] = lax.dot_general(v, probs_low, head, preferred_element_type=f32).astype(low).T
    qg_ref[0] = lax.dot_general(k, ds, head, preferred_element_type=f32).astype(low).T
    kg = jnp.dot(ds, q, preferred_element_type=f32)
    vg = jnp.dot(probs_low, g, preferred_element_type=f32)
    kg_ref[:, 0] = kg.reshape(n, r, e).astype(low)
    vg_ref[:, 0] = vg.reshape(n, r, e).astype(low)


VM = pl.BlockSpec(memory_space=pltpu.VMEM)
BIG = 60 * 1024 * 1024


def per_device(n, m, all_features, video_query, text_states, key_weight, value_weight, text_lengths, output_grad):
    samples, rows, features = video_query.shape
    _, r, depth = text_states.shape
    heads = features // HEAD
    low, f32 = jnp.bfloat16, jnp.float32
    Z, Y, C = n // 4, 2, 2
    dma = pltpu.SemaphoreType.DMA
    k_loc = jnp.dot(text_states, key_weight, preferred_element_type=f32).astype(low)
    v_loc = jnp.dot(text_states, value_weight, preferred_element_type=f32).astype(low)
    spread6 = jax.ShapeDtypeStruct((Z, Y, C, samples, r, features), low)
    k_full, v_full, cols = pl.pallas_call(
        functools.partial(gather_kernel, n),
        out_shape=(spread6, spread6, jax.ShapeDtypeStruct((n, samples, r, depth // n), low)),
        in_specs=[VM] * 3,
        out_specs=(VM,) * 3,
        scratch_shapes=[dma((2, 4 * Z - 1)), dma((2, 4 * Z - 1)), dma((n - 1,)), dma((n - 1,))],
        compiler_params=pltpu.CompilerParams(
            collective_id=0, has_side_effects=True, vmem_limit_bytes=BIG
        ),
        name="gather_kv",
    )(k_loc, v_loc, text_states)
    text_spec = pl.BlockSpec((n, 1, r, HEAD), lambda b, h, s: (0, b, 0, h))
    video_spec = pl.BlockSpec((1, rows, HEAD), lambda b, h, s: (b, 0, h))
    video_out = jax.ShapeDtypeStruct(video_query.shape, low)
    text_out = jax.ShapeDtypeStruct((n, samples, r, features), low)
    attended, query_grad, kg, vg = pl.pallas_call(
        functools.partial(attention_kernel, 1.0 / math.sqrt(HEAD)),
        out_shape=(video_out, video_out, text_out, text_out),
        grid_spec=pltpu.PrefetchScalarGridSpec(
            num_scalar_prefetch=1,
            grid=(samples, heads),
            in_specs=[video_spec, text_spec, text_spec, video_spec],
            out_specs=(video_spec, video_spec, text_spec, text_spec),
        ),
        compiler_params=pltpu.CompilerParams(vmem_limit_bytes=32 * 1024 * 1024),
        name="attention",
    )(
        text_lengths,
        video_query,
        k_full.reshape(n, samples, r, features),
        v_full.reshape(n, samples, r, features),
        output_grad,
    )
    six = (Z, Y, C, samples, r, features)
    five = (Z, Y, samples, r, features)
    four = (Z, samples, r, features)
    vmem = pltpu.VMEM
    cuts = 2 * (2 if features % 256 == 0 else 1)
    tk, tv = pl.pallas_call(
        functools.partial(reduce_kernel, n),
        out_shape=(spread6, spread6),
        in_specs=[VM] * 2,
        out_specs=(VM,) * 2,
        scratch_shapes=[
            vmem(five, low), vmem(five, low), vmem(five, low), vmem(five, low),
            vmem(four, low), vmem(four, low), vmem(four, low), vmem(four, low),
            vmem((Z - 1,) + four[1:], low), vmem((Z - 1,) + four[1:], low),
            vmem(four[1:], low), vmem(four[1:], low),
            dma((cuts, Z + 1)), dma((cuts, Z + 1)),
            dma((cuts, 4 * Z - 1)), dma((cuts, 4 * Z - 1)),
        ],
        compiler_params=pltpu.CompilerParams(
            collective_id=1, has_side_effects=True, vmem_limit_bytes=BIG
        ),
        name="reduce_grads",
    )(kg.reshape(six), vg.reshape(six))
    cols = cols.reshape(n * samples * r, depth // n)
    over = (((0,), (0,)), ((), ()))
    key_raw = lax.dot_general(
        cols, tk.reshape(n * samples * r, features), over, preferred_element_type=f32
    )
    value_raw = lax.dot_general(
        cols, tv.reshape(n * samples * r, features), over, preferred_element_type=f32
    )
    squares = jnp.sum(key_raw * key_raw) + jnp.sum(value_raw * value_raw)
    parts = pl.pallas_call(
        functools.partial(scalar_kernel, n, m),
        out_shape=jax.ShapeDtypeStruct((n * m, 8, 128), f32),
        in_specs=[VM],
        out_specs=VM,
        scratch_shapes=[dma((n * m - 1,)), dma((n * m - 1,))],
        compiler_params=pltpu.CompilerParams(collective_id=2, has_side_effects=True),
        name="scalar_sum",
    )(jnp.broadcast_to(squares, (8, 128)))
    overall = jnp.sum(parts[:, 0, 0])
    spread = jnp.sqrt(overall / (2.0 * depth * all_features) + 1e-06)
    factor = 1.0 / jnp.maximum(spread, 1.0)
    return attended, query_grad, key_raw * factor, value_raw * factor


def solution(mesh):
    n, m = mesh.shape["seq"], mesh.shape["tp"]
    in_specs = (
        P(None, "seq", "tp"),
        P(None, "seq", None),
        P(None, "tp"),
        P(None, "tp"),
        P(),
        P(None, "seq", "tp"),
    )
    out_specs = (P(None, "seq", "tp"), P(None, "seq", "tp"), P("seq", "tp"), P("seq", "tp"))

    def step(*args):
        body = functools.partial(per_device, n, m, args[0].shape[2])
        return jax.shard_map(
            body, mesh=mesh, in_specs=in_specs, out_specs=out_specs, check_vma=False
        )(*args)

    return step
```

time: 352 us -> 164 us (0.47)
  Pallas kernels: 0 us -> 134 us
  waiting for transfers between devices: 125 us -> 0 us
  matrix products: 104 us -> 14.7 us
  blocking collectives: 58.1 us -> 0 us
  local copies, waits for them, and re-layouts: 42.1 us -> 8.34 us
  between operations: 14.9 us -> 2.75 us
    pallas_call x0 -> x4, Pallas kernels: none -> 134 us  [the longest x1 61.2 us: per_device(): pl.pallas_call(functools.partial(reduce_kernel, n), out_shape=(spread6, s...]
    dot_general x9 -> x4, matrix products: 92 us -> 14.7 us  [the longest x1 7.61 us: per_device(): jnp.dot(text_states, key_weight, preferred_element_type=f32).astype(low)]
    psum x1 -> x0, waiting for transfers between devices: 77 us -> none  [per_device(): key_total, value_total = lax.psum((key_grad, value_grad), 'seq')]
    all_gather x1 -> x0, waiting for transfers between devices: 47.5 us -> none  [per_device(): text_full = lax.all_gather(text_states, 'seq', axis=1, tiled=True)]
    psum x1 -> x0, blocking collectives: 40.4 us -> none  [per_device(): overall = lax.psum(squares, ('seq', 'tp'))]
    unnamed x19 -> x22, local copies, waits for them, and re-layouts: 29.5 us -> 7.74 us
    all_to_all x1 -> x0, blocking collectives: 17.7 us -> none  [per_device(): lax.all_to_all(text_states, 'seq', split_axis=2, concat_axis=1, tiled=True)]
    sub x1 -> x0, matrix products: 12.2 us -> none  [per_device(): weights = jnp.exp(scores - highest)]
  transfers between devices with their start and end apart: 2 -> 0, of which waited for: 2 -> 0; matrix products, arithmetic and copies ran while one was open for 16% -> 0% of each run, Pallas kernels for 0% -> 0%
where the time goes in v1:
time: 164 us; the launch traced here: 163 us
  Pallas kernels  134 us (82%)
  matrix products  14.7 us (9%)
  local copies, waits for them, and re-layouts  8.34 us (5%)
  other arithmetic  3.45 us (2%)
  between operations  2.75 us (2%)
    pallas_call x1, Pallas kernels, per_device(): pl.pallas_call(functools.partial(reduce_kernel, n), out_shape=(spread6, s...  61.2 us
    pallas_call x1, Pallas kernels, per_device(): pl.pallas_call(functools.partial(gather_kernel, n), out_shape=(spread6, s...  39.3 us
    pallas_call x1, Pallas kernels, per_device(): pl.pallas_call(functools.partial(attention_kernel, 1.0 / math.sqrt(HEAD))...  24 us
    pallas_call x1, Pallas kernels, per_device(): pl.pallas_call(functools.partial(scalar_kernel, n, m), out_shape=jax.Shap...  9.47 us
    unnamed x22, local copies, waits for them, and re-layouts  7.74 us
    dot_general x1, matrix products, per_device(): jnp.dot(text_states, key_weight, preferred_element_type=f32).astype(low)  7.61 us

profile of v1, /device:TPU:0, one launch (start us, length us, event | category | flops | bytes accessed | tf_op | source)
XLA Modules:
  0.0 163.3 jit_solution(1638827117440434166)
XLA Ops:
  0.6 0.0 copy-start.8
  0.6 0.0 copy-start.7
  0.7 7.6 %fusion.4.k_loc = bf16[2,16,1536]{2,1,0:T(8,128)(2,1)} fusion(bf16[2,16,4096]{2,1,0:T(8,128)(2,1)} %text.1, bf16[4096,1536]{1,0:T(8,128)(2,1)} %param.8), kind=kOutput, calls=%fused_computation.4 | convolution fusion | flops 402702336 | bytes 12943360 | tf_op jit(solution)/shard_map/dot_general | solution.py:290
  8.3 0.0 copy-done.8
  8.3 0.7 copy-done.7
  9.0 0.0 copy-start
  9.0 0.0 copy-start.6
  9.0 2.8 %fusion.7.v_loc = bf16[2,16,1536]{2,1,0:T(8,128)(2,1)} fusion(bf16[2,16,4096]{2,1,0:T(8,128)(2,1)S(1)} %copy-done.8, bf16[4096,1536]{1,0:T(8,128)(2,1)S(1)} %copy-done.7), kind=kOutput, calls=%fused_computation.5 | convolution fusion | flops 402702336 | bytes 12943360 | tf_op jit(solution)/shard_map/dot_general | solution.py:291
  11.8 39.3 %gather_kv.1 = (bf16[4,2,2,2,16,1536]{5,4,3,2,1,0:T(8,128)(2,1)}, bf16[4,2,2,2,16,1536]{5,4,3,2,1,0:T(8,128)(2,1)}, bf16[16,2,16,256]{3,2,1,0:T(8,128)(2,1)}) custom-call(bf16[2,16,1536]{2,1,0:T(8,128)(2,1)} %fusion.4.k_loc, bf16[2,16,1536]{2,1,0:T(8,128)(2,1)} %fusion.7.v_loc, bf16[2,16,4096]{2,1,0:T(8,128)(2,1)} %text.1), custom_call_target="tpu_custom_call" | custom-call | tf_op jit(solution)/shard_map/gather_kv/pallas_call | solution.py:293
  51.1 0.0 copy-done
  51.1 0.0 copy-done.6
  51.1 0.0 copy-start.1
  51.1 1.9 %copy-done.1 = bf16[2,512,1536]{2,1,0:T(8,128)(2,1)S(1)} copy-done((bf16[2,512,1536]{2,1,0:T(8,128)(2,1)S(1)}, bf16[2,512,1536]{2,1,0:T(8,128)(2,1)}, u32[]{:S(2)}) %copy-start.1) | copy-done | bytes 3145752
  53.0 0.0 copy-start.2
  53.0 1.4 copy-done.2
  54.4 0.0 copy-start.3
  54.4 1.4 copy-done.3
  55.8 24.0 %attention.1 = (bf16[2,512,1536]{2,1,0:T(8,128)(2,1)}, bf16[2,512,1536]{2,1,0:T(8,128)(2,1)}, bf16[16,2,16,1536]{3,2,1,0:T(8,128)(2,1)S(1)}, bf16[16,2,16,1536]{3,2,1,0:T(8,128)(2,1)S(1)}) custom-call(s32[2]{0:T(128)S(1)} %copy-done.6, bf16[2,512,1536]{2,1,0:T(8,128)(2,1)S(1)} %copy-done, bf16[16,2,16,1536]{3,2,1,0:T(8,128)(2,1)S(1)} %bitcast.23, ...), custom_call_target="tpu_custom_call" | custom-call | tf_op jit(solution)/shard_map/attention/pallas_call | solution.py:308
  79.8 0.0 copy-start.4
  79.8 1.1 copy-done.4
  81.0 0.0 copy-start.5
  81.0 1.1 copy-done.5
  82.1 0.0 copy-start.10
  82.1 61.2 %reduce_grads.1 = (bf16[4,2,2,2,16,1536]{5,4,3,2,1,0:T(8,128)(2,1)}, bf16[4,2,2,2,16,1536]{5,4,3,2,1,0:T(8,128)(2,1)}) custom-call(bf16[4,2,2,2,16,1536]{5,4,3,2,1,0:T(8,128)(2,1)} %bitcast.25, bf16[4,2,2,2,16,1536]{5,4,3,2,1,0:T(8,128)(2,1)} %bitcast.26), custom_call_target="tpu_custom_call" | custom-call | tf_op jit(solution)/shard_map/reduce_grads/pallas_call | solution.py:331
  143.4 0.0 copy-done.10
  143.4 0.0 copy-start.9
  143.4 2.9 %multiply_reduce_fusion = (f32[]{:T(128)}, f32[256,1536]{1,0:T(8,128)S(1)}) fusion(bf16[512,256]{1,0:T(8,128)(2,1)S(1)} %bitcast.29, bf16[512,1536]{1,0:T(8,128)(2,1)} %bitcast.28), kind=kOutput, calls=%fused_computation.6 | convolution fusion | flops 403439616 | bytes 3407876 | tf_op jit(solution)/shard_map/dot_general | solution.py:354
  146.3 0.0 copy-done.9
  146.3 1.4 multiply_reduce_fusion.1
  149.0 0.6 broadcast_in_dim.3.x
  149.6 9.5 %scalar_sum.1 = f32[32,8,128]{2,1,0:T(8,128)} custom-call(f32[8,128]{1,0:T(8,128)} %broadcast_in_dim.3.x), custom_call_target="tpu_custom_call" | custom-call | tf_op jit(solution)/shard_map/scalar_sum/pallas_call | solution.py:358
  159.1 1.5 slice_reduce_fusion
  161.4 1.9 %broadcast_multiply_fusion = (f32[256,1536]{1,0:T(8,128)}, f32[256,1536]{1,0:T(8,128)}) fusion(f32[256,1536]{1,0:T(8,128)S(1)} %get-tuple-element.25, f32[]{:T(128)S(6)} %div.7, f32[256,1536]{1,0:T(8,128)S(1)} %get-tuple-element.23), kind=kLoop, calls=%fused_computation.8 | loop fusion | flops 786432 | bytes 6291460 | tf_op jit(solution)/shard_map/mul | solution.py:370
Async XLA Ops:
  0.6 7.6 %copy-start.8 = (bf16[2,16,4096]{2,1,0:T(8,128)(2,1)S(1)}, bf16[2,16,4096]{2,1,0:T(8,128)(2,1)}, u32[]{:S(2)}) copy-start(bf16[2,16,4096]{2,1,0:T(8,128)(2,1)} %text.1) | copy-start | bytes 786436
  0.6 8.4 %copy-start.7 = (bf16[4096,1536]{1,0:T(8,128)(2,1)S(1)}, bf16[4096,1536]{1,0:T(8,128)(2,1)}, u32[]{:S(2)}) copy-start(bf16[4096,1536]{1,0:T(8,128)(2,1)} %param.9) | copy-start | bytes 37748740
  9.0 42.1 %copy-start = (bf16[2,512,1536]{2,1,0:T(8,128)(2,1)S(1)}, bf16[2,512,1536]{2,1,0:T(8,128)(2,1)}, u32[]{:S(2)}) copy-start(bf16[2,512,1536]{2,1,0:T(8,128)(2,1)} %q_ref.1) | copy-start | bytes 9437188
  9.0 42.1 %copy-start.6 = (s32[2]{0:T(128)S(1)}, s32[2]{0:T(128)}, u32[]{:S(2)}) copy-start(s32[2]{0:T(128)} %lengths.1) | copy-start | bytes 28
  51.1 1.9 %copy-start.1 = (bf16[2,512,1536]{2,1,0:T(8,128)(2,1)S(1)}, bf16[2,512,1536]{2,1,0:T(8,128)(2,1)}, u32[]{:S(2)}) copy-start(bf16[2,512,1536]{2,1,0:T(8,128)(2,1)} %g_ref.1) | copy-start | bytes 9437188
  53.0 1.4 copy-start.2
  54.4 1.4 copy-start.3
  79.8 1.1 copy-start.4
  81.0 1.1 copy-start.5
  82.1 61.2 %copy-start.10 = (bf16[16,2,16,256]{3,2,1,0:T(8,128)(2,1)S(1)}, bf16[16,2,16,256]{3,2,1,0:T(8,128)(2,1)}, u32[]{:S(2)}) copy-start(bf16[16,2,16,256]{3,2,1,0:T(8,128)(2,1)} %get-tuple-element.17) | copy-start | bytes 786436
  143.4 2.9 %copy-start.9 = (bf16[4,2,2,2,16,1536]{5,4,3,2,1,0:T(8,128)(2,1)S(1)}, bf16[4,2,2,2,16,1536]{5,4,3,2,1,0:T(8,128)(2,1)}, u32[]{:S(2)}) copy-start(bf16[4,2,2,2,16,1536]{5,4,3,2,1,0:T(8,128)(2,1)} %get-tuple-element.20) | copy-start | bytes 4718596

commit v2 on v0

v2 whole, which is shorter than its diff:
```python
import functools
import math

import jax
import jax.numpy as jnp
from jax import lax
from jax.experimental import pallas as pl
from jax.experimental.pallas import tpu as pltpu
from jax.sharding import PartitionSpec as P

HEAD = 128
MESH = pl.DeviceIdType.MESH
NEG = -1e30


def rem(a, b):
    return lax.rem(a, b)


class Place:
    def __init__(self, n):
        self.C = 2
        self.Y = 2
        self.Z = n // 4
        self.n = n
        me = lax.axis_index("seq")
        self.me = me
        self.tp = lax.axis_index("tp")
        self.c = rem(me, 2)
        self.y = rem(me // 2, 2)
        self.z = me // 4

    def dev(self, z, y, c):
        return ((z * self.Y + y) * self.C + c, self.tp)

    def core_peer(self):
        return self.dev(self.z, self.y, 1 - self.c)

    def y_peer(self):
        return self.dev(self.z, 1 - self.y, self.c)

    def z_ahead(self, d):
        return rem(self.z + d, self.Z)

    def z_behind(self, d):
        return rem(self.z + self.Z - d, self.Z)

    def z_peer(self, d):
        return self.dev(self.z_ahead(d), self.y, self.c)


def rcopy(src, dst, ssem, rsem, dev):
    return pltpu.make_async_remote_copy(
        src_ref=src, dst_ref=dst, send_sem=ssem, recv_sem=rsem, device_id=dev, device_id_type=MESH
    )


def greet(devices):
    barrier = pltpu.get_barrier_semaphore()
    for d in devices:
        pl.semaphore_signal(barrier, inc=1, device_id=d, device_id_type=MESH)
    pl.semaphore_wait(barrier, len(devices))


class Gather:
    def __init__(self, pos, block, own, ss, rs):
        self.pos, self.block, self.own, self.ss, self.rs = pos, block, own, ss, rs
        self.sent = []

    def copy(self, src, z, y, c, k, dev):
        d = rcopy(src, self.block(z, y, c), self.ss(k), self.rs(k), dev)
        return d

    def go(self, src, z, y, c, k, dev):
        d = self.copy(src, z, y, c, k, dev)
        d.start()
        self.sent.append(d)

    def start(self):
        p = self.pos
        for d in range(p.Z - 1, 0, -1):
            self.go(self.own, p.z, p.y, p.c, d - 1, p.z_peer(d))
        self.go(self.own, p.z, p.y, p.c, p.Z - 1, p.y_peer())
        self.go(self.own, p.z, p.y, p.c, 2 * p.Z - 1, p.core_peer())

    def arrive_z(self, d):
        p = self.pos
        self.sent[p.Z - 1 - d].wait_recv()
        zz = p.z_behind(d)
        self.go(self.block(zz, p.y, p.c), zz, p.y, p.c, p.Z - 1 + d, p.y_peer())
        self.go(self.block(zz, p.y, p.c), zz, p.y, p.c, 2 * p.Z - 1 + d, p.core_peer())

    def arrive_y(self, d):
        p = self.pos
        zz = p.z_behind(d)
        src = self.block(zz, 1 - p.y, p.c)
        rcopy(src, src, self.ss(p.Z - 1 + d), self.rs(p.Z - 1 + d), p.y_peer()).wait_recv()
        self.go(src, zz, 1 - p.y, p.c, 3 * p.Z - 1 + d, p.core_peer())

    def arrive_core(self):
        p = self.pos
        for d in range(2 * p.Z):
            k = 2 * p.Z - 1 + d
            src = self.own
            rcopy(src, src, self.ss(k), self.rs(k), p.core_peer()).wait_recv()

    def drain(self):
        for d in self.sent:
            d.wait_send()


def flat_rows(x):
    e = x.shape[-1]
    if x.shape[-2] % 16 == 0:
        return x.reshape(-1, e)
    return x.astype(jnp.float32).reshape(-1, e).astype(x.dtype)


def attend(scaling, length, q, g, k, v):
    f32, low = jnp.float32, jnp.bfloat16
    last = (((1,), (1,)), ((), ()))
    head = (((0,), (0,)), ((), ()))
    s = lax.dot_general(k, q, last, preferred_element_type=f32)
    dp = lax.dot_general(v, g, last, preferred_element_type=f32)
    row = lax.broadcasted_iota(jnp.int32, s.shape, 0)
    s = jnp.where(row < length, s, NEG)
    top = jnp.max(s, axis=0, keepdims=True)
    w = jnp.exp2((s - top) * (scaling * math.log2(math.e)))
    inv = 1.0 / jnp.sum(w, axis=0, keepdims=True)
    probs = w * inv
    probs_low = probs.astype(low)
    delta = jnp.sum(probs * dp, axis=0, keepdims=True)
    ds = (probs * (dp - delta) * scaling).astype(low)
    attended = lax.dot_general(v, probs_low, head, preferred_element_type=f32).astype(low).T
    query_grad = lax.dot_general(k, ds, head, preferred_element_type=f32).astype(low).T
    key_grad = jnp.dot(ds, q, preferred_element_type=f32)
    value_grad = jnp.dot(probs_low, g, preferred_element_type=f32)
    return attended, query_grad, key_grad, value_grad


def layer_kernel(n, m, groups, scaling, lengths, kv_loc, text, q_hbm, g_hbm, a_hbm, qg_hbm, raw, parts,
                 q, g, a, qg, kv, grads, s1, r1, s2, r2, r3, own, total, cols, cols_t, mine,
                 local, ks, kr, ts, tr, ss, rs, gs, gr, ps, pr):
    f32, low = jnp.float32, jnp.bfloat16
    p = Place(n)
    Z, Y, C = p.Z, p.Y, p.C
    samples, _, features = q.shape
    r = text.shape[1]
    width = cols.shape[-1]
    wide = features // groups
    heads = wide // HEAD
    part = [pl.ds(i * wide, wide) for i in range(groups)]
    loads = [
        pltpu.make_async_copy(q_hbm, q, local.at[0]),
        pltpu.make_async_copy(g_hbm, g, local.at[1]),
    ]
    for cp in loads:
        cp.start()
    flat = p.me * m + p.tp
    peers = []
    for d in range(1, n * m):
        to = rem(flat + d, n * m)
        peers.append((to // m, rem(to, m)))
    greet(peers)

    inward = []
    for i, w in enumerate(part):
        f = Gather(
            p,
            lambda z, y, c, w=w: kv.at[z, y, c, :, :, :, w],
            kv_loc.at[:, :, :, w],
            lambda k, i=i: ks.at[i, k],
            lambda k, i=i: kr.at[i, k],
        )
        f.start()
        inward.append(f)
    direct = []
    for d in range(1, n):
        to = rem(p.me + d, n)
        start = pl.multiple_of(to * width, 128)
        cp = rcopy(
            text.at[:, :, pl.ds(start, width)], cols.at[p.me], ts.at[d - 1], tr.at[d - 1], (to, p.tp)
        )
        cp.start()
        direct.append(cp)
    kv[p.z, p.y, p.c] = kv_loc[...]
    cols[p.me] = text[:, :, pl.ds(pl.multiple_of(p.me * width, 128), width)]

    def in_z(i):
        for d in range(1, Z):
            inward[i].arrive_z(d)

    def in_y(i):
        for d in range(Z):
            inward[i].arrive_y(d)

    def unit(i, b):
        length = lengths[b]

        def one(h, carry):
            w = pl.ds(pl.multiple_of((i * heads + h) * HEAD, HEAD), HEAD)
            k = flat_rows(kv[:, :, :, 0, b, :, w])
            v = flat_rows(kv[:, :, :, 1, b, :, w])
            att, q_grad, k_grad, v_grad = attend(scaling, length, q[b, :, w], g[b, :, w], k, v)
            a[b, :, w] = att
            qg[b, :, w] = q_grad
            grads[:, :, :, 0, b, :, w] = k_grad.reshape(Z, Y, C, r, HEAD).astype(low)
            grads[:, :, :, 1, b, :, w] = v_grad.reshape(Z, Y, C, r, HEAD).astype(low)
            return carry

        lax.fori_loop(0, heads, one, 0)

    sends, stores, outward = [], [], {}
    hold = {}

    def core_send(i):
        w = part[i]
        cp = rcopy(
            grads.at[:, :, 1 - p.c, :, :, :, w], r1.at[:, :, :, :, :, w], ss.at[i, 0], rs.at[i, 0],
            p.core_peer(),
        )
        cp.start()
        sends.append(cp)
        hold[i, 0] = cp
        for src, dst, k in ((a, a_hbm, 0), (qg, qg_hbm, 1)):
            st = pltpu.make_async_copy(src.at[:, :, w], dst.at[:, :, w], local.at[2 + 2 * i + k])
            st.start()
            stores.append(st)

    def core_sum(i):
        w = part[i]
        hold[i, 0].wait_recv()
        for far in (True, False):
            yy = 1 - p.y if far else p.y
            s1[:, yy, :, :, :, w] = (
                grads[:, yy, p.c, :, :, :, w].astype(f32) + r1[:, yy, :, :, :, w].astype(f32)
            ).astype(low)
            if far:
                cp = rcopy(
                    s1.at[:, yy, :, :, :, w], r2.at[:, :, :, :, w], ss.at[i, 1], rs.at[i, 1], p.y_peer()
                )
                cp.start()
                sends.append(cp)
                hold[i, 1] = cp

    def y_sum(i):
        w = part[i]
        hold[i, 1].wait_recv()
        for d in range(Z - 1, 0, -1):
            zz = p.z_ahead(d)
            s2[zz, :, :, :, w] = (
                s1[zz, p.y, :, :, :, w].astype(f32) + r2[zz, :, :, :, w].astype(f32)
            ).astype(low)
            cp = rcopy(
                s2.at[zz, :, :, :, w], r3.at[d - 1, :, :, :, w], ss.at[i, 1 + d], rs.at[i, 1 + d],
                p.z_peer(d),
            )
            cp.start()
            sends.append(cp)
            hold[i, 1 + d] = cp

    def z_sum(i):
        w = part[i]
        x = s1[p.z, p.y, :, :, :, w].astype(f32) + r2[p.z, :, :, :, w].astype(f32)
        for d in range(1, Z):
            hold[i, 1 + d].wait_recv()
            x = x + r3[d - 1, :, :, :, w].astype(f32)
        own[:, :, :, w] = x.astype(low)
        f = Gather(
            p,
            lambda z, y, c: total.at[z, y, c, :, :, :, w],
            own.at[:, :, :, w],
            lambda k: gs.at[i, k],
            lambda k: gr.at[i, k],
        )
        f.start()
        total[p.z, p.y, p.c, :, :, :, w] = x.astype(low)
        outward[i] = f

    def out_z(i):
        for d in range(1, Z):
            outward[i].arrive_z(d)

    def out_y(i):
        for d in range(Z):
            outward[i].arrive_y(d)

    squares = []

    def out_core(i):
        if i == 0:
            for cp in direct:
                cp.wait_recv()
            cols_t[...] = flat_rows(cols[...]).T
        outward[i].arrive_core()
        for kind in range(2):
            x = flat_rows(total[:, :, :, kind, :, :, part[i]])
            y = jnp.dot(cols_t[...], x, preferred_element_type=f32)
            raw[kind, :, part[i]] = y
            squares.append(jnp.sum((y * y).reshape(-1, 8, wide), axis=0))

    stages = (core_sum, y_sum, z_sum, out_z, out_y, out_core)
    pending = {}

    def turn():
        for i in sorted(pending):
            stages[pending[i]](i)
            pending[i] += 1
            if pending[i] == len(stages):
                del pending[i]

    in_z(0)
    in_y(0)
    if groups > 1:
        in_z(1)
    inward[0].arrive_core()
    for cp in loads:
        cp.wait()
    for i in range(groups):
        for b in range(samples):
            unit(i, b)
            if b == 0:
                if i + 1 < groups:
                    in_y(i + 1)
                if i + 2 < groups:
                    in_z(i + 2)
                turn()
        core_send(i)
        if i + 1 < groups:
            inward[i + 1].arrive_core()
        turn()
        pending[i] = 0
    while pending:
        turn()
    acc = squares[0]
    for x in squares[1:]:
        acc = acc + x
    mine[...] = jnp.broadcast_to(jnp.sum(acc, keepdims=True), mine.shape)
    last = []
    for d, dev in enumerate(peers):
        cp = rcopy(mine, parts.at[flat], ps.at[d], pr.at[d], dev)
        cp.start()
        last.append(cp)
    parts[flat] = mine[...]
    for st in stores:
        st.wait()
    for f in inward:
        f.drain()
    for i in sorted(outward):
        outward[i].drain()
    for cp in direct + sends:
        cp.wait_send()
    for cp in last:
        cp.wait()


VM = pl.BlockSpec(memory_space=pltpu.VMEM)
ANY = pl.BlockSpec(memory_space=pl.ANY)
BIG = 58 * 1024 * 1024


def per_device(n, m, all_features, video_query, text_states, key_weight, value_weight, text_lengths, output_grad):
    samples, rows, features = video_query.shape
    _, r, depth = text_states.shape
    heads = features // HEAD
    groups = 4 if heads % 4 == 0 else (3 if heads % 3 == 0 else 1)
    low, f32 = jnp.bfloat16, jnp.float32
    Z, Y, C = n // 4, 2, 2
    dma, vmem = pltpu.SemaphoreType.DMA, pltpu.VMEM
    k_loc = jnp.dot(text_states, key_weight, preferred_element_type=f32).astype(low)
    v_loc = jnp.dot(text_states, value_weight, preferred_element_type=f32).astype(low)
    kv_loc = jnp.stack((k_loc, v_loc))
    block = (2, samples, r, features)
    full = vmem((Z, Y, C) + block, low)
    half = vmem((Z, Y) + block, low)
    quarter = vmem((Z,) + block, low)
    video = vmem(video_query.shape, low)
    video_out = jax.ShapeDtypeStruct(video_query.shape, low)
    g_sems = (groups, 4 * Z - 1)
    attended, query_grad, raw, parts = pl.pallas_call(
        functools.partial(layer_kernel, n, m, groups, 1.0 / math.sqrt(HEAD)),
        out_shape=(
            video_out,
            video_out,
            jax.ShapeDtypeStruct((2, depth // n, features), f32),
            jax.ShapeDtypeStruct((n * m, 8, 128), f32),
        ),
        in_specs=[pl.BlockSpec(memory_space=pltpu.SMEM), VM, VM, ANY, ANY],
        out_specs=(ANY, ANY, VM, VM),
        scratch_shapes=[
            video, video, video, video,
            full, full, half, half, quarter, quarter, vmem((Z - 1,) + block, low), vmem(block, low), full,
            vmem((n, samples, r, depth // n), low), vmem((depth // n, n * samples * r), low),
            vmem((8, 128), f32),
            dma((2 + 2 * groups,)),
            dma(g_sems), dma(g_sems), dma((n - 1,)), dma((n - 1,)),
            dma((groups, Z + 1)), dma((groups, Z + 1)), dma(g_sems), dma(g_sems),
            dma((n * m - 1,)), dma((n * m - 1,)),
        ],
        compiler_params=pltpu.CompilerParams(
            collective_id=0, has_side_effects=True, vmem_limit_bytes=BIG
        ),
        name="layer",
    )(text_lengths, kv_loc, text_states, video_query, output_grad)
    overall = jnp.sum(parts[:, 0, 0])
    spread = jnp.sqrt(overall / (2.0 * depth * all_features) + 1e-06)
    factor = 1.0 / jnp.maximum(spread, 1.0)
    return attended, query_grad, raw[0] * factor, raw[1] * factor


def solution(mesh):
    n, m = mesh.shape["seq"], mesh.shape["tp"]
    in_specs = (
        P(None, "seq", "tp"),
        P(None, "seq", None),
        P(None, "tp"),
        P(None, "tp"),
        P(),
        P(None, "seq", "tp"),
    )
    out_specs = (P(None, "seq", "tp"), P(None, "seq", "tp"), P("seq", "tp"), P("seq", "tp"))

    def step(*args):
        body = functools.partial(per_device, n, m, args[0].shape[2])
        return jax.shard_map(
            body, mesh=mesh, in_specs=in_specs, out_specs=out_specs, check_vma=False
        )(*args)

    return step
```

time: 352 us -> 127 us (0.36)
  waiting for transfers between devices: 125 us -> 0 us
  Pallas kernels: 0 us -> 104 us
  matrix products: 104 us -> 9.11 us
  blocking collectives: 58.1 us -> 0 us
  local copies, waits for them, and re-layouts: 42.1 us -> 6.05 us
  between operations: 14.9 us -> 1.41 us
    pallas_call x0 -> x1, Pallas kernels: none -> 104 us  [per_device(): pl.pallas_call(functools.partial(layer_kernel, n, m, groups, 1.0 / math.s...]
    dot_general x9 -> x2, matrix products: 92 us -> 9.11 us  [the longest x1 6.95 us: per_device(): jnp.dot(text_states, key_weight, preferred_element_type=f32).astype(low)]
    psum x1 -> x0, waiting for transfers between devices: 77 us -> none  [per_device(): key_total, value_total = lax.psum((key_grad, value_grad), 'seq')]
    all_gather x1 -> x0, waiting for transfers between devices: 47.5 us -> none  [per_device(): text_full = lax.all_gather(text_states, 'seq', axis=1, tiled=True)]
    psum x1 -> x0, blocking collectives: 40.4 us -> none  [per_device(): overall = lax.psum(squares, ('seq', 'tp'))]
    unnamed x19 -> x10, local copies, waits for them, and re-layouts: 29.5 us -> 6.05 us
    all_to_all x1 -> x0, blocking collectives: 17.7 us -> none  [per_device(): lax.all_to_all(text_states, 'seq', split_axis=2, concat_axis=1, tiled=True)]
    sub x1 -> x0, matrix products: 12.2 us -> none  [per_device(): weights = jnp.exp(scores - highest)]
  transfers between devices with their start and end apart: 2 -> 0, of which waited for: 2 -> 0; matrix products, arithmetic and copies ran while one was open for 16% -> 0% of each run, Pallas kernels for 0% -> 0%
where the time goes in v2:
time: 127 us
  Pallas kernels  104 us (82%)
  matrix products  9.11 us (7%)
  other arithmetic  6.19 us (5%)
  local copies, waits for them, and re-layouts  6.05 us (5%)
  between operations  1.41 us (1%)
    pallas_call x1, Pallas kernels, per_device(): pl.pallas_call(functools.partial(layer_kernel, n, m, groups, 1.0 / math.s...  104 us
    dot_general x1, matrix products, per_device(): jnp.dot(text_states, key_weight, preferred_element_type=f32).astype(low)  6.95 us
    unnamed x10, local copies, waits for them, and re-layouts  6.05 us
    mul x1, other arithmetic, per_device(): return (attended, query_grad, raw[0] * factor, raw[1] * factor)  3.94 us

profile of v2, /device:TPU:0, one launch (start us, length us, event | category | flops | bytes accessed | tf_op | source)
XLA Modules:
  0.0 126.6 jit_solution(10870345496285262576)
XLA Ops:
  0.6 0.0 copy-start.3
  0.6 0.0 copy-start
  0.7 7.0 %fusion.13 = bf16[1,2,16,1536]{3,2,1,0:T(8,128)(2,1)S(1)} fusion(bf16[2,16,4096]{2,1,0:T(8,128)(2,1)} %text.1, bf16[4096,1536]{1,0:T(8,128)(2,1)} %param.8), kind=kOutput, calls=%fused_computation.7 | convolution fusion | flops 402702336 | bytes 12943360 | tf_op jit(solution)/shard_map/dot_general | solution.py:370
  7.6 0.0 copy-done.3
  7.6 1.3 %copy-done = bf16[4096,1536]{1,0:T(8,128)(2,1)S(1)} copy-done((bf16[4096,1536]{1,0:T(8,128)(2,1)S(1)}, bf16[4096,1536]{1,0:T(8,128)(2,1)}, u32[]{:S(2)}) %copy-start) | copy-done | bytes 12582936
  9.0 2.2 %fusion.10 = bf16[1,2,16,1536]{3,2,1,0:T(8,128)(2,1)S(1)} fusion(bf16[2,16,4096]{2,1,0:T(8,128)(2,1)S(1)} %copy-done.3, bf16[4096,1536]{1,0:T(8,128)(2,1)S(1)} %copy-done), kind=kOutput, calls=%fused_computation.6 | convolution fusion | flops 402702336 | bytes 12943360 | tf_op jit(solution)/shard_map/dot_general | solution.py:371
  11.1 0.7 pad_maximum_fusion.kv_loc
  11.8 103.8 %layer.1 = (bf16[2,512,1536]{2,1,0:T(8,128)(2,1)}, bf16[2,512,1536]{2,1,0:T(8,128)(2,1)}, f32[2,256,1536]{2,1,0:T(8,128)}, f32[32,8,128]{2,1,0:T(8,128)}) custom-call(s32[2]{0:T(128)} %lengths.1, bf16[2,2,16,1536]{3,2,1,0:T(8,128)(2,1)} %pad_maximum_fusion.kv_loc, bf16[2,16,4096]{2,1,0:T(8,128)(2,1)} %text.1, bf16[2,512,1536]{2,1,0:T(8,128)(2,1)} %q_hbm.1, ...), custom_call_target="tpu_custom_call" | custom-call | tf_op jit(solution)/shard_map/layer/pallas_call | solution.py:380
  115.6 1.5 %slice_reduce_fusion = f32[]{:T(128)} fusion(f32[32,8,128]{2,1,0:T(8,128)} %get-tuple-element.11), kind=kLoop, calls=%fused_computation.11 | loop fusion | flops 31 | bytes 132 | tf_op jit(solution)/shard_map/reduce_sum | solution.py:405
  117.9 0.0 copy-start.2
  117.9 3.9 %multiply_bitcast_fusion = (f32[256,1536]{1,0:T(8,128)}, f32[256,1536]{1,0:T(8,128)}) fusion(f32[2,256,1536]{2,1,0:T(8,128)} %get-tuple-element.10, f32[]{:T(128)S(6)} %div.7), kind=kLoop, calls=%fused_computation.8 | loop fusion | flops 786432 | bytes 6291460 | tf_op jit(solution)/shard_map/mul | solution.py:408
  121.9 0.0 copy-done.2
  121.9 0.0 copy-start.1
  121.9 1.7 %copy.12 = bf16[2,512,1536]{2,1,0:T(8,128)(2,1)} copy(bf16[2,512,1536]{2,1,0:T(8,128)(2,1)S(1)} %copy-done.2) | data formatting | bytes 6291456
  123.5 1.4 %copy-done.1 = bf16[2,512,1536]{2,1,0:T(8,128)(2,1)S(1)} copy-done((bf16[2,512,1536]{2,1,0:T(8,128)(2,1)S(1)}, bf16[2,512,1536]{2,1,0:T(8,128)(2,1)}, u32[]{:S(2)}) %copy-start.1) | copy-done | bytes 3145752
  124.9 1.7 %copy.13 = bf16[2,512,1536]{2,1,0:T(8,128)(2,1)} copy(bf16[2,512,1536]{2,1,0:T(8,128)(2,1)S(1)} %copy-done.1) | data formatting | bytes 6291456
Async XLA Ops:
  0.6 7.0 %copy-start.3 = (bf16[2,16,4096]{2,1,0:T(8,128)(2,1)S(1)}, bf16[2,16,4096]{2,1,0:T(8,128)(2,1)}, u32[]{:S(2)}) copy-start(bf16[2,16,4096]{2,1,0:T(8,128)(2,1)} %text.1) | copy-start | bytes 786436
  0.6 8.3 %copy-start = (bf16[4096,1536]{1,0:T(8,128)(2,1)S(1)}, bf16[4096,1536]{1,0:T(8,128)(2,1)}, u32[]{:S(2)}) copy-start(bf16[4096,1536]{1,0:T(8,128)(2,1)} %param.9) | copy-start | bytes 37748740
  117.9 4.0 %copy-start.2 = (bf16[2,512,1536]{2,1,0:T(8,128)(2,1)S(1)}, bf16[2,512,1536]{2,1,0:T(8,128)(2,1)}, u32[]{:S(2)}) copy-start(bf16[2,512,1536]{2,1,0:T(8,128)(2,1)} %get-tuple-element.18) | copy-start | bytes 9437188
  121.9 3.0 %copy-start.1 = (bf16[2,512,1536]{2,1,0:T(8,128)(2,1)S(1)}, bf16[2,512,1536]{2,1,0:T(8,128)(2,1)}, u32[]{:S(2)}) copy-start(bf16[2,512,1536]{2,1,0:T(8,128)(2,1)} %get-tuple-element.19) | copy-start | bytes 9437188

commit v3 on v2

--- a/solution.py
+++ b/solution.py
@@ -138,7 +138,7 @@
     return attended, query_grad, key_grad, value_grad
 
 
-def layer_kernel(n, m, groups, scaling, lengths, kv_loc, text, q_hbm, g_hbm, a_hbm, qg_hbm, raw, parts,
+def layer_kernel(n, m, groups, scaling, count, lengths, kv_loc, text, q_hbm, g_hbm, a_hbm, qg_hbm, raw, factor, parts,
                  q, g, a, qg, kv, grads, s1, r1, s2, r2, r3, own, total, cols, cols_t, mine,
                  local, ks, kr, ts, tr, ss, rs, gs, gr, ps, pr):
     f32, low = jnp.float32, jnp.bfloat16
@@ -352,11 +352,13 @@
         cp.wait_send()
     for cp in last:
         cp.wait()
+    spread = jnp.sqrt(jnp.sum(parts[...], axis=0) / count + 1e-06)
+    factor[...] = 1.0 / jnp.maximum(spread, 1.0)
 
 
 VM = pl.BlockSpec(memory_space=pltpu.VMEM)
 ANY = pl.BlockSpec(memory_space=pl.ANY)
-BIG = 58 * 1024 * 1024
+BIG = 40 * 1024 * 1024
 
 
 def per_device(n, m, all_features, video_query, text_states, key_weight, value_weight, text_lengths, output_grad):
@@ -377,17 +379,19 @@
     video = vmem(video_query.shape, low)
     video_out = jax.ShapeDtypeStruct(video_query.shape, low)
     g_sems = (groups, 4 * Z - 1)
-    attended, query_grad, raw, parts = pl.pallas_call(
-        functools.partial(layer_kernel, n, m, groups, 1.0 / math.sqrt(HEAD)),
+    count = 2.0 * depth * all_features
+    attended, query_grad, raw, factor = pl.pallas_call(
+        functools.partial(layer_kernel, n, m, groups, 1.0 / math.sqrt(HEAD), count),
         out_shape=(
             video_out,
             video_out,
             jax.ShapeDtypeStruct((2, depth // n, features), f32),
-            jax.ShapeDtypeStruct((n * m, 8, 128), f32),
+            jax.ShapeDtypeStruct((8, 128), f32),
         ),
         in_specs=[pl.BlockSpec(memory_space=pltpu.SMEM), VM, VM, ANY, ANY],
         out_specs=(ANY, ANY, VM, VM),
         scratch_shapes=[
+            vmem((n * m, 8, 128), f32),
             video, video, video, video,
             full, full, half, half, quarter, quarter, vmem((Z - 1,) + block, low), vmem(block, low), full,
             vmem((n, samples, r, depth // n), low), vmem((depth // n, n * samples * r), low),
@@ -402,9 +406,7 @@
         ),
         name="layer",
     )(text_lengths, kv_loc, text_states, video_query, output_grad)
-    overall = jnp.sum(parts[:, 0, 0])
-    spread = jnp.sqrt(overall / (2.0 * depth * all_features) + 1e-06)
-    factor = 1.0 / jnp.maximum(spread, 1.0)
+    factor = factor[0, 0]
     return attended, query_grad, raw[0] * factor, raw[1] * factor
 
 

time: 127 us -> 120 us (0.945)
  other arithmetic: 6.19 us -> 2.57 us
  Pallas kernels: 104 us -> 102 us
    pallas_call x1, Pallas kernels: 104 us -> 102 us  [per_device(): pl.pallas_call(functools.partial(layer_kernel, n, m, groups, 1.0 / math.s...]
    reduce_sum x1 -> x0, other arithmetic: 1.54 us -> none  [per_device(): overall = jnp.sum(parts[:, 0, 0])]
    mul x1, other arithmetic: 3.94 us -> 2.55 us  [per_device(): return (attended, query_grad, raw[0] * factor, raw[1] * factor)]
    unnamed x10, local copies, waits for them, and re-layouts: 6.05 us -> 4.69 us
where the time goes in v3:
time: 120 us; the launch traced here: 119 us
  Pallas kernels  102 us (85%)
  matrix products  9.1 us (8%)
  local copies, waits for them, and re-layouts  5.21 us (4%)
  other arithmetic  2.57 us (2%)
    pallas_call x1, Pallas kernels, per_device(): pl.pallas_call(functools.partial(layer_kernel, n, m, groups, 1.0 / math.s...  102 us
    dot_general x1, matrix products, per_device(): jnp.dot(text_states, key_weight, preferred_element_type=f32).astype(low)  6.95 us
    unnamed x10, local copies, waits for them, and re-layouts  4.69 us
    mul x1, other arithmetic, per_device(): return (attended, query_grad, raw[0] * factor, raw[1] * factor)  2.55 us

profile of v3, /device:TPU:0, one launch (start us, length us, event | category | flops | bytes accessed | tf_op | source)
XLA Modules:
  0.0 119.5 jit_solution(6842812728918504296)
XLA Ops:
  0.6 0.0 copy-start.1
  0.6 0.0 copy-start.3
  0.7 6.9 %fusion.13 = bf16[1,2,16,1536]{3,2,1,0:T(8,128)(2,1)S(1)} fusion(bf16[2,16,4096]{2,1,0:T(8,128)(2,1)} %text.1, bf16[4096,1536]{1,0:T(8,128)(2,1)} %param.8), kind=kOutput, calls=%fused_computation.7 | convolution fusion | flops 402702336 | bytes 12943360 | tf_op jit(solution)/shard_map/dot_general | solution.py:372
  7.6 0.0 copy-done.1
  7.6 1.3 %copy-done.3 = bf16[4096,1536]{1,0:T(8,128)(2,1)S(1)} copy-done((bf16[4096,1536]{1,0:T(8,128)(2,1)S(1)}, bf16[4096,1536]{1,0:T(8,128)(2,1)}, u32[]{:S(2)}) %copy-start.3) | copy-done | bytes 12582936
  9.0 0.0 copy-start
  9.0 0.0 copy-start.2
  9.0 2.2 %fusion.10 = bf16[1,2,16,1536]{3,2,1,0:T(8,128)(2,1)S(1)} fusion(bf16[2,16,4096]{2,1,0:T(8,128)(2,1)S(1)} %copy-done.1, bf16[4096,1536]{1,0:T(8,128)(2,1)S(1)} %copy-done.3), kind=kOutput, calls=%fused_computation.6 | convolution fusion | flops 402702336 | bytes 12943360 | tf_op jit(solution)/shard_map/dot_general | solution.py:373
  11.2 0.0 copy-done
  11.2 0.0 copy-done.2
  11.2 101.9 %layer.1 = (bf16[2,512,1536]{2,1,0:T(8,128)(2,1)S(1)}, bf16[2,512,1536]{2,1,0:T(8,128)(2,1)S(1)}, f32[2,256,1536]{2,1,0:T(8,128)S(1)}, f32[8,128]{1,0:T(8,128)S(1)}) custom-call(s32[2]{0:T(128)S(1)} %copy-done.2, bf16[2,2,16,1536]{3,2,1,0:T(8,128)(2,1)S(1)} %pad_maximum_fusion.kv_loc, bf16[2,16,4096]{2,1,0:T(8,128)(2,1)S(1)} %copy-done.1, ...), custom_call_target="tpu_custom_call" | custom-call | tf_op jit(solution)/shard_map/layer/pallas_call | solution.py:383
  113.1 0.5 slice.10
  113.6 2.5 %multiply_bitcast_fusion = (f32[256,1536]{1,0:T(8,128)}, f32[256,1536]{1,0:T(8,128)}) fusion(f32[2,256,1536]{2,1,0:T(8,128)S(1)} %get-tuple-element.10, f32[]{:T(128)} %bitcast.4), kind=kLoop, calls=%fused_computation.8 | loop fusion | flops 786432 | bytes 6291460 | tf_op jit(solution)/shard_map/mul | solution.py:410
  116.2 1.7 %copy.12 = bf16[2,512,1536]{2,1,0:T(8,128)(2,1)} copy(bf16[2,512,1536]{2,1,0:T(8,128)(2,1)S(1)} %get-tuple-element.18) | data formatting | bytes 6291456
  117.8 1.7 %copy.13 = bf16[2,512,1536]{2,1,0:T(8,128)(2,1)} copy(bf16[2,512,1536]{2,1,0:T(8,128)(2,1)S(1)} %get-tuple-element.19) | data formatting | bytes 6291456
  (1 shorter events, 0.0 us)
Async XLA Ops:
  0.6 7.0 %copy-start.1 = (bf16[2,16,4096]{2,1,0:T(8,128)(2,1)S(1)}, bf16[2,16,4096]{2,1,0:T(8,128)(2,1)}, u32[]{:S(2)}) copy-start(bf16[2,16,4096]{2,1,0:T(8,128)(2,1)} %text.1) | copy-start | bytes 786436
  0.6 8.3 %copy-start.3 = (bf16[4096,1536]{1,0:T(8,128)(2,1)S(1)}, bf16[4096,1536]{1,0:T(8,128)(2,1)}, u32[]{:S(2)}) copy-start(bf16[4096,1536]{1,0:T(8,128)(2,1)} %param.9) | copy-start | bytes 37748740
  9.0 2.2 %copy-start = (bf16[2,512,1536]{2,1,0:T(8,128)(2,1)S(1)}, bf16[2,512,1536]{2,1,0:T(8,128)(2,1)}, u32[]{:S(2)}) copy-start(bf16[2,512,1536]{2,1,0:T(8,128)(2,1)} %q_hbm.1) | copy-start | bytes 9437188
  9.0 2.2 %copy-start.2 = (s32[2]{0:T(128)S(1)}, s32[2]{0:T(128)}, u32[]{:S(2)}) copy-start(s32[2]{0:T(128)} %lengths.1) | copy-start | bytes 28
